TPU v7x, 32 devices: a whole 2x2x4 slice. The times are simulated.
32 devices in a mesh: ex: 8 (over y, x, core), tp: 4 (over z).
Axes of the slice: x: 2, y: 2, z: 4, core: 2. Of those that a mesh axis runs over, the one named last changes fastest.
Arguments:
- samples: bfloat16 [192, 2048], P(('ex', 'tp')), may hold values from -6 to 6
- gate_weight: bfloat16 [2048, 44], replicated, may hold values from -15 to 15
- up_weight: bfloat16 [16, 2048, 4096], P('ex', None, 'tp'), may hold values from -0.125 to 0.125
- down_weight: bfloat16 [16, 4096, 2048], P('ex', 'tp'), may hold values from -0.09375 to 0.09375
Outputs:
- task_outputs: bfloat16 [192, 5, 2048], P(('ex', 'tp'))
All inputs are finite; a program needn't handle non-finite values.
Results may differ from a plain program's by a relative error of at most 0.0055.
Values may be sent and summed in bfloat16 or wider, within the bound.
A program may use at most 128 MiB of HBM per device.

v0:
```python
import jax
import jax.numpy as jnp
import numpy as np
from jax import lax
from jax.sharding import PartitionSpec as P

TASKS = 4
TASK_EXP = 3
SHARED = 4
EXPERTS = 16
GATES = 44


def routing_table():
    per_task = TASK_EXP + SHARED
    table = np.zeros((GATES, (TASKS + 1) * EXPERTS), np.float32)
    for task_idx in range(TASKS):
        for column in range(per_task):
            if column < TASK_EXP:
                expert_idx = task_idx * TASK_EXP + column
            else:
                expert_idx = TASKS * TASK_EXP + column - TASK_EXP
            table[task_idx * per_task + column, task_idx * EXPERTS + expert_idx] = 1.0
    for expert_idx in range(EXPERTS):
        table[TASKS * per_task + expert_idx, TASKS * EXPERTS + expert_idx] = 1.0
    return jnp.asarray(table, dtype=jnp.float32)


def gate_mix(rows, gate_weight):
    logits = jnp.dot(rows, gate_weight, preferred_element_type=jnp.float32)
    per_task = TASK_EXP + SHARED
    pieces = []
    for task_idx in range(TASKS):
        pieces.append(
            jax.nn.softmax(logits[:, task_idx * per_task : (task_idx + 1) * per_task], axis=-1)
        )
    pieces.append(jax.nn.softmax(logits[:, TASKS * per_task :], axis=-1))
    probs = jnp.concatenate(pieces, axis=1)
    mixed = jnp.dot(probs, routing_table(), precision=lax.Precision.HIGHEST)
    return mixed.reshape(rows.shape[0], TASKS + 1, EXPERTS)


def on_device(samples, gate_weight, up_weight, down_weight):
    local_experts = up_weight.shape[0]
    ex_count = lax.axis_size("ex")
    tp_count = lax.axis_size("tp")
    row_dev = samples.shape[0]
    width = samples.shape[1]
    piece = lax.all_gather(samples, ("ex", "tp"), axis=0, tiled=True)
    outputs = []
    for expert_idx in range(local_experts):
        outputs.append(
            jnp.maximum(
                jnp.dot(piece, up_weight[expert_idx], preferred_element_type=jnp.float32), 0.0
            ).astype(jnp.bfloat16)
        )
    hidden = jnp.stack(outputs, axis=1)
    partial_out = jnp.einsum(
        "rlf,lfd->rld", hidden, down_weight, preferred_element_type=jnp.float32
    )
    blocked = partial_out.reshape(ex_count, tp_count * row_dev, local_experts, width)
    summed = lax.psum_scatter(blocked, "tp", scatter_dimension=1, tiled=True)
    gathered = lax.all_to_all(summed, "ex", split_axis=0, concat_axis=2, tiled=True)[0]
    mixing = gate_mix(samples, gate_weight)
    result = jnp.einsum("rke,red->rkd", mixing, gathered, precision=lax.Precision.HIGHEST)
    return result.astype(jnp.bfloat16)


def solution(mesh):
    placed = (P(("ex", "tp"), None), P(), P("ex", None, "tp"), P("ex", "tp", None))
    return jax.shard_map(
        on_device,
        mesh=mesh,
        in_specs=placed,
        out_specs=P(("ex", "tp"), None, None),
        check_vma=False,
    )
```

profile of v0, /device:TPU:0, one launch (start us, length us, event | category | flops | bytes accessed | tf_op | source)
XLA Modules:
  0.0 185.9 jit_solution(10094937951658092538)
XLA Ops:
  6.5 0.0 copy-start
  6.5 0.0 reduce-scatter.2.cloned.1.call-start
  6.5 78.9 %all-gather = bf16[32,6,2048]{2,1,0:T(8,128)(2,1)S(1)} all-gather(bf16[1,6,2048]{2,1,0:T(8,128)(2,1)} %bitcast.43), channel_id=1, replica_groups=mesh['ex'=8,'tp'=4] {'ex','tp'}, dimensions={0}, use_global_device_ids=true | all-gather | bytes 811008 | tf_op jit(solution)/shard_map/all_gather | solution.py:49
  85.5 0.3 reshape.20
  85.7 3.2 %fusion.21 = bf16[192,1,1024]{2,0,1:T(8,128)(2,1)S(1)} fusion(bf16[192,2048]{1,0:T(8,128)(2,1)S(1)} %reshape.20, bf16[2,2048,1024]{2,1,0:T(8,128)(2,1)} %param.7), kind=kOutput, calls=%fused_computation.12 | convolution fusion | flops 805699584 | bytes 5373952 | tf_op jit(solution)/shard_map/dot_general | solution.py:54
  88.9 3.2 %fusion.18 = bf16[192,1,1024]{2,0,1:T(8,128)(2,1)S(1)} fusion(bf16[192,2048]{1,0:T(8,128)(2,1)S(1)} %reshape.20, bf16[2,2048,1024]{2,1,0:T(8,128)(2,1)} %param.7), kind=kOutput, calls=%fused_computation.11 | convolution fusion | flops 805699584 | bytes 5373952 | tf_op jit(solution)/shard_map/dot_general | solution.py:54
  92.1 5.2 %fusion.24 = f32[2,192,2048]{2,1,0:T(8,128)S(1)} fusion(bf16[2,1024,2048]{2,1,0:T(8,128)(2,1)} %param.8, bf16[192,1,1024]{2,0,1:T(8,128)(2,1)S(1)} %fusion.21, bf16[192,1,1024]{2,0,1:T(8,128)(2,1)S(1)} %fusion.18), kind=kOutput, calls=%fused_computation.17 | convolution fusion | flops 1611005952 | bytes 12320768 | tf_op jit(solution)/shard_map/rlf,lfd->rld/dot_general | solution.py:58
  97.3 0.0 copy-start.1
  97.3 0.0 copy-start.5
  97.3 0.0 copy-start.6
  97.3 0.0 copy-start.4
  97.3 0.0 copy-start.3
  97.3 0.0 copy-start.2
  97.4 3.5 %copy.10 = f32[8,24,2,2048]{3,0,2,1:T(8,128)} copy(f32[8,24,2,2048]{3,1,0,2:T(8,128)S(1)} %bitcast.41) | data formatting | bytes 6291456 | tf_op jit(solution)/shard_map/reshape | solution.py:61
  100.8 0.0 reduce-scatter.2.cloned.1.call-update
  100.9 0.0 copy-done
  100.9 0.0 copy-done.1
  100.9 0.2 fusion.50
  101.0 0.2 slice_reduce_fusion
  101.2 0.2 slice_reduce_fusion.1
  101.5 0.2 fusion.37
  101.7 0.0 copy-done.5
  101.7 0.2 fusion.31
  101.9 0.0 copy-done.6
  101.9 0.2 convolution_add_fusion.3
  102.1 56.2 %reduce-scatter.2.cloned.1.call-done = f32[8,6,2,2048]{3,0,2,1:T(8,128)} async-done(((f32[8,24,2,2048]{3,0,2,1:T(8,128)}), f32[8,6,2,2048]{3,0,2,1:T(8,128)}) %reduce-scatter.2.cloned.1.call-update) | async-done | bytes 786448 | tf_op jit(solution)/shard_map/reduce_scatter | solution.py:62
  158.3 2.6 %copy.11 = f32[8,6,2,2048]{3,2,1,0:T(2,128)} copy(f32[8,6,2,2048]{3,0,2,1:T(8,128)} %reduce-scatter.2.cloned.1.call-done) | data formatting | bytes 1572864 | tf_op jit(solution)/shard_map/reduce_scatter | solution.py:62
  161.0 3.6 %all-to-all-start = ((f32[8,6,2,2048]{3,2,1,0:T(2,128)}), f32[8,6,2,2048]{3,2,1,0:T(2,128)S(1)}, u32[]{:S(2)}, u32[]{:S(2)}) async-start(f32[8,6,2,2048]{3,2,1,0:T(2,128)} %copy.11), calls=%async_computation.1 | async-start | bytes 1572864 | tf_op jit(solution)/shard_map/all_to_all | solution.py:63
  164.6 0.2 fusion.38
  164.8 0.0 copy-done.4
  164.8 0.2 convolution_add_fusion.2
  165.0 0.0 copy-done.3
  165.0 0.2 convolution_add_fusion.1
  165.2 0.0 copy-done.2
  165.2 0.2 convolution_add_fusion
  165.4 0.1 reshape.17
  165.5 11.7 %all-to-all-done = f32[8,6,2,2048]{3,2,1,0:T(2,128)S(1)} async-done(((f32[8,6,2,2048]{3,2,1,0:T(2,128)}), f32[8,6,2,2048]{3,2,1,0:T(2,128)S(1)}, u32[]{:S(2)}, u32[]{:S(2)}) %all-to-all-start) | async-done | bytes 786464 | tf_op jit(solution)/shard_map/all_to_all | solution.py:63
  177.2 0.1 copy.12
  177.2 0.5 squeeze.11
  177.8 0.5 convolution_convert_fusion
  178.3 0.8 copy.13
Async XLA Ops:
  6.5 94.3 %copy-start = (bf16[2048,44]{0,1:T(8,128)(2,1)S(1)}, bf16[2048,44]{0,1:T(8,128)(2,1)}, u32[]{:S(2)}) copy-start(bf16[2048,44]{0,1:T(8,128)(2,1)} %param.6) | copy-start | bytes 540676
  6.5 151.8 %reduce-scatter.2.cloned.1.call-start = ((), (), s32[]{:S(2)}) async-start(), calls=%async_computation.2 | async-start | bytes 3932160 | tf_op jit(solution)/shard_map/reduce_scatter | solution.py:62
  97.3 3.6 %copy-start.1 = (bf16[6,2048]{1,0:T(8,128)(2,1)S(1)}, bf16[6,2048]{1,0:T(8,128)(2,1)}, u32[]{:S(2)}) copy-start(bf16[6,2048]{1,0:T(8,128)(2,1)} %param.5) | copy-start | bytes 73732
  97.3 4.4 %copy-start.5 = (f32[7,80]{1,0:T(8,128)S(1)}, f32[7,80]{1,0:T(8,128)}, u32[]{:S(2)}) copy-start(f32[7,80]{1,0:T(8,128)} %constant.12) | copy-start | bytes 6724
  97.3 4.6 %copy-start.6 = (f32[7,80]{1,0:T(8,128)S(1)}, f32[7,80]{1,0:T(8,128)}, u32[]{:S(2)}) copy-start(f32[7,80]{1,0:T(8,128)} %constant.13) | copy-start | bytes 6724
  97.3 67.5 %copy-start.4 = (f32[7,80]{1,0:T(8,128)S(1)}, f32[7,80]{1,0:T(8,128)}, u32[]{:S(2)}) copy-start(f32[7,80]{1,0:T(8,128)} %constant.14) | copy-start | bytes 6724
  97.3 67.7 %copy-start.3 = (f32[7,80]{1,0:T(8,128)S(1)}, f32[7,80]{1,0:T(8,128)}, u32[]{:S(2)}) copy-start(f32[7,80]{1,0:T(8,128)} %constant.15) | copy-start | bytes 6724
  97.3 67.9 %copy-start.2 = (f32[16,80]{1,0:T(8,128)S(1)}, f32[16,80]{1,0:T(8,128)}, u32[]{:S(2)}) copy-start(f32[16,80]{1,0:T(8,128)} %constant.16) | copy-start | bytes 15364
  161.0 16.2 %all-to-all-start = ((f32[8,6,2,2048]{3,2,1,0:T(2,128)}), f32[8,6,2,2048]{3,2,1,0:T(2,128)S(1)}, u32[]{:S(2)}, u32[]{:S(2)}) async-start(f32[8,6,2,2048]{3,2,1,0:T(2,128)} %copy.11), calls=%async_computation.1 | async-start | bytes 1572864 | tf_op jit(solution)/shard_map/all_to_all | solution.py:63
Sparse Core Ops, SparseCore 0:
  101.0 57.3 reduce-scatter.1
where the time goes:
time: 186 us
  blocking collectives  78.9 us (42%)
  waiting for transfers between devices  67.9 us (37%)
  between operations  13.5 us (7%)
  matrix products  13.2 us (7%)
  local copies, waits for them, and re-layouts  7.84 us (4%)
  starting transfers between devices  3.65 us (2%)
    all_gather x1, blocking collectives, on_device(): piece = lax.all_gather(samples, ('ex', 'tp'), axis=0, tiled=True)  78.9 us
    reduce_scatter x1, waiting for transfers between devices, on_device(): summed = lax.psum_scatter(blocked, 'tp', scatter_dimension=1, tiled=True)  56.2 us
    all_to_all x1, waiting for transfers between devices, on_device(): lax.all_to_all(summed, 'ex', split_axis=0, concat_axis=2, tiled=True)[0]  11.7 us
    dot_general x2, matrix products, on_device(): jnp.dot(piece, up_weight[expert_idx], preferred_element_type=jnp.float32)  6.35 us
    dot_general x1, matrix products, on_device(): jnp.einsum('rlf,lfd->rld', hidden, down_weight, preferred_element_type=jn...  5.18 us
  transfers between devices with their start and end apart: 2, of which 2 were waited for; matrix products, arithmetic and copies ran while one was open for 1% of the time, Pallas kernels for 0%

commit v1 on v0

--- a/solution.py
+++ b/solution.py
@@ -1,3 +1,4 @@
+import functools
 import jax
 import jax.numpy as jnp
 import numpy as np
@@ -9,6 +10,19 @@
 SHARED = 4
 EXPERTS = 16
 GATES = 44
+
+
+def types_divide(local_values, axis_name):
+    full_n = lax.axis_size(axis_name)
+    pool = []
+    for k0 in tuple(range(local_values.ndim)):
+        pool.append(full_n if k0 == 0 else 1)
+    answer = jnp.tile(local_values, pool)
+    kept_arr = lax.all_to_all(answer, axis_name=axis_name, split_axis=0, concat_axis=0, tiled=True)
+    return kept_arr
+
+
+reach_thing_here = functools.partial(types_divide, axis_name=("ex", "tp"))
 
 
 def routing_table():
@@ -46,7 +60,7 @@
     tp_count = lax.axis_size("tp")
     row_dev = samples.shape[0]
     width = samples.shape[1]
-    piece = lax.all_gather(samples, ("ex", "tp"), axis=0, tiled=True)
+    piece = reach_thing_here(samples)
     outputs = []
     for expert_idx in range(local_experts):
         outputs.append(

time: 186 us -> 143 us (0.77)
  blocking collectives: 78.9 us -> 32.1 us
  waiting for transfers between devices: 67.9 us -> 71 us
    all_gather x1 -> x0, blocking collectives: 78.9 us -> none  [on_device(): piece = lax.all_gather(samples, ('ex', 'tp'), axis=0, tiled=True)]
    all_to_all x0 -> x1, blocking collectives: none -> 32.1 us  [types_divide(): lax.all_to_all(answer, axis_name=axis_name, split_axis=0, concat_axis=0,...]
    reduce_scatter x1, waiting for transfers between devices: 56.2 us -> 59.3 us  [on_device(): summed = lax.psum_scatter(blocked, 'tp', scatter_dimension=1, tiled=True)]
where the time goes in v1:
time: 143 us
  waiting for transfers between devices  71 us (50%)
  blocking collectives  32.1 us (22%)
  between operations  13.5 us (9%)
  matrix products  13.2 us (9%)
  local copies, waits for them, and re-layouts  8.74 us (6%)
  starting transfers between devices  3.66 us (3%)
    reduce_scatter x1, waiting for transfers between devices, on_device(): summed = lax.psum_scatter(blocked, 'tp', scatter_dimension=1, tiled=True)  59.3 us
    all_to_all x1, blocking collectives, types_divide(): lax.all_to_all(answer, axis_name=axis_name, split_axis=0, concat_axis=0,...  32.1 us
    all_to_all x1, waiting for transfers between devices, on_device(): lax.all_to_all(summed, 'ex', split_axis=0, concat_axis=2, tiled=True)[0]  11.7 us
    dot_general x2, matrix products, on_device(): jnp.dot(piece, up_weight[expert_idx], preferred_element_type=jnp.float32)  6.35 us
    dot_general x1, matrix products, on_device(): jnp.einsum('rlf,lfd->rld', hidden, down_weight, preferred_element_type=jn...  5.18 us
    all_to_all x1, starting transfers between devices, on_device(): lax.all_to_all(summed, 'ex', split_axis=0, concat_axis=2, tiled=True)[0]  3.65 us
    reshape x1, local copies, waits for them, and re-layouts, on_device(): partial_out.reshape(ex_count, tp_count * row_dev, local_experts, width)  3.49 us
  transfers between devices with their start and end apart: 2, of which 2 were waited for; matrix products, arithmetic and copies ran while one was open for 1% of the time, Pallas kernels for 0%

profile of v1, /device:TPU:0, one launch (start us, length us, event | category | flops | bytes accessed | tf_op | source)
XLA Modules:
  0.0 143.1 jit_solution(15946620488880686702)
XLA Ops:
  6.5 0.0 copy-start
  6.5 0.0 reduce-scatter.2.cloned.1.call-start
  6.5 0.9 tile.2
  7.5 32.1 %all_to_all.24 = bf16[32,6,2048]{2,1,0:T(8,128)(2,1)S(1)} all-to-all(bf16[32,6,2048]{2,1,0:T(8,128)(2,1)S(1)} %tile.2), channel_id=1, replica_groups=mesh['ex'=8,'tp'=4] {'ex','tp'}, dimensions={0} | all-to-all | bytes 1572864 | tf_op jit(solution)/shard_map/all_to_all | solution.py:21
  39.5 0.3 all_to_all.18
  39.8 3.2 %fusion.21 = bf16[192,1,1024]{2,0,1:T(8,128)(2,1)S(1)} fusion(bf16[192,2048]{1,0:T(8,128)(2,1)S(1)} %all_to_all.18, bf16[2,2048,1024]{2,1,0:T(8,128)(2,1)} %param.7), kind=kOutput, calls=%fused_computation.12 | convolution fusion | flops 805699584 | bytes 5373952 | tf_op jit(solution)/shard_map/dot_general | solution.py:68
  43.0 3.2 %fusion.18 = bf16[192,1,1024]{2,0,1:T(8,128)(2,1)S(1)} fusion(bf16[192,2048]{1,0:T(8,128)(2,1)S(1)} %all_to_all.18, bf16[2,2048,1024]{2,1,0:T(8,128)(2,1)} %param.7), kind=kOutput, calls=%fused_computation.11 | convolution fusion | flops 805699584 | bytes 5373952 | tf_op jit(solution)/shard_map/dot_general | solution.py:68
  46.1 5.2 %fusion.24 = f32[2,192,2048]{2,1,0:T(8,128)S(1)} fusion(bf16[2,1024,2048]{2,1,0:T(8,128)(2,1)} %param.8, bf16[192,1,1024]{2,0,1:T(8,128)(2,1)S(1)} %fusion.21, bf16[192,1,1024]{2,0,1:T(8,128)(2,1)S(1)} %fusion.18), kind=kOutput, calls=%fused_computation.17 | convolution fusion | flops 1611005952 | bytes 12320768 | tf_op jit(solution)/shard_map/rlf,lfd->rld/dot_general | solution.py:72
  51.3 0.0 copy-start.1
  51.3 0.0 copy-start.5
  51.4 0.0 copy-start.6
  51.4 0.0 copy-start.4
  51.4 0.0 copy-start.3
  51.4 0.0 copy-start.2
  51.4 3.5 %copy.10 = f32[8,24,2,2048]{3,0,2,1:T(8,128)} copy(f32[8,24,2,2048]{3,1,0,2:T(8,128)S(1)} %bitcast.40) | data formatting | bytes 6291456 | tf_op jit(solution)/shard_map/reshape | solution.py:75
  54.9 0.0 reduce-scatter.2.cloned.1.call-update
  54.9 0.0 copy-done
  54.9 0.0 copy-done.1
  54.9 0.2 fusion.50
  55.1 0.2 slice_reduce_fusion
  55.3 0.2 slice_reduce_fusion.1
  55.5 0.2 fusion.37
  55.8 0.0 copy-done.5
  55.8 0.2 fusion.31
  56.0 0.0 copy-done.6
  56.0 0.2 convolution_add_fusion.3
  56.2 59.3 %reduce-scatter.2.cloned.1.call-done = f32[8,6,2,2048]{3,0,2,1:T(8,128)} async-done(((f32[8,24,2,2048]{3,0,2,1:T(8,128)}), f32[8,6,2,2048]{3,0,2,1:T(8,128)}) %reduce-scatter.2.cloned.1.call-update) | async-done | bytes 786448 | tf_op jit(solution)/shard_map/reduce_scatter | solution.py:76
  115.5 2.6 %copy.11 = f32[8,6,2,2048]{3,2,1,0:T(2,128)} copy(f32[8,6,2,2048]{3,0,2,1:T(8,128)} %reduce-scatter.2.cloned.1.call-done) | data formatting | bytes 1572864 | tf_op jit(solution)/shard_map/reduce_scatter | solution.py:76
  118.1 3.7 %all-to-all-start.1 = ((f32[8,6,2,2048]{3,2,1,0:T(2,128)}), f32[8,6,2,2048]{3,2,1,0:T(2,128)S(1)}, u32[]{:S(2)}, u32[]{:S(2)}) async-start(f32[8,6,2,2048]{3,2,1,0:T(2,128)} %copy.11), calls=%async_computation.2 | async-start | bytes 1572864 | tf_op jit(solution)/shard_map/all_to_all | solution.py:77
  121.8 0.2 fusion.38
  122.0 0.0 copy-done.4
  122.0 0.2 convolution_add_fusion.2
  122.2 0.0 copy-done.3
  122.2 0.2 convolution_add_fusion.1
  122.4 0.0 copy-done.2
  122.4 0.2 convolution_add_fusion
  122.6 0.1 reshape.24
  122.7 11.7 %all-to-all-done.1 = f32[8,6,2,2048]{3,2,1,0:T(2,128)S(1)} async-done(((f32[8,6,2,2048]{3,2,1,0:T(2,128)}), f32[8,6,2,2048]{3,2,1,0:T(2,128)S(1)}, u32[]{:S(2)}, u32[]{:S(2)}) %all-to-all-start.1) | async-done | bytes 786464 | tf_op jit(solution)/shard_map/all_to_all | solution.py:77
  134.3 0.1 copy.12
  134.4 0.5 squeeze.11
  135.0 0.5 convolution_convert_fusion
  135.5 0.8 copy.13
Async XLA Ops:
  6.5 48.4 %copy-start = (bf16[2048,44]{0,1:T(8,128)(2,1)S(1)}, bf16[2048,44]{0,1:T(8,128)(2,1)}, u32[]{:S(2)}) copy-start(bf16[2048,44]{0,1:T(8,128)(2,1)} %param.6) | copy-start | bytes 540676
  6.5 109.0 %reduce-scatter.2.cloned.1.call-start = ((), (), s32[]{:S(2)}) async-start(), calls=%async_computation.3 | async-start | bytes 3932160 | tf_op jit(solution)/shard_map/reduce_scatter | solution.py:76
  51.3 3.6 %copy-start.1 = (bf16[6,2048]{1,0:T(8,128)(2,1)S(1)}, bf16[6,2048]{1,0:T(8,128)(2,1)}, u32[]{:S(2)}) copy-start(bf16[6,2048]{1,0:T(8,128)(2,1)} %param.5) | copy-start | bytes 73732
  51.3 4.4 %copy-start.5 = (f32[7,80]{1,0:T(8,128)S(1)}, f32[7,80]{1,0:T(8,128)}, u32[]{:S(2)}) copy-start(f32[7,80]{1,0:T(8,128)} %constant.12) | copy-start | bytes 6724
  51.4 4.6 %copy-start.6 = (f32[7,80]{1,0:T(8,128)S(1)}, f32[7,80]{1,0:T(8,128)}, u32[]{:S(2)}) copy-start(f32[7,80]{1,0:T(8,128)} %constant.13) | copy-start | bytes 6724
  51.4 70.6 %copy-start.4 = (f32[7,80]{1,0:T(8,128)S(1)}, f32[7,80]{1,0:T(8,128)}, u32[]{:S(2)}) copy-start(f32[7,80]{1,0:T(8,128)} %constant.14) | copy-start | bytes 6724
  51.4 70.8 %copy-start.3 = (f32[7,80]{1,0:T(8,128)S(1)}, f32[7,80]{1,0:T(8,128)}, u32[]{:S(2)}) copy-start(f32[7,80]{1,0:T(8,128)} %constant.15) | copy-start | bytes 6724
  51.4 71.0 %copy-start.2 = (f32[16,80]{1,0:T(8,128)S(1)}, f32[16,80]{1,0:T(8,128)}, u32[]{:S(2)}) copy-start(f32[16,80]{1,0:T(8,128)} %constant.16) | copy-start | bytes 15364
  118.1 16.2 %all-to-all-start.1 = ((f32[8,6,2,2048]{3,2,1,0:T(2,128)}), f32[8,6,2,2048]{3,2,1,0:T(2,128)S(1)}, u32[]{:S(2)}, u32[]{:S(2)}) async-start(f32[8,6,2,2048]{3,2,1,0:T(2,128)} %copy.11), calls=%async_computation.2 | async-start | bytes 1572864 | tf_op jit(solution)/shard_map/all_to_all | solution.py:77
Sparse Core Ops, SparseCore 0:
  55.0 60.4 reduce-scatter.1
